TPU v7x, 32 devices: a whole 2x2x4 slice. The times are simulated.
32 devices in a mesh: grp: 4 (over y, x), dev: 8 (over z, core).
Axes of the slice: x: 2, y: 2, z: 4, core: 2. Of those that a mesh axis runs over, the one named last changes fastest.
Arguments:
- leaf_emit: float32 [3, 4096], P(None, 'dev'), may hold values from 0 to 1
- leaf_albedo: float32 [3, 4096], P(None, 'dev'), may hold values from 0.2 to 0.9
- leaf_radiosity: float32 [3, 4096], P(None, 'dev'), may hold values from 0.05 to 4
- leaf_area: float32 [4096], P('dev'), may hold values from 0.002 to 0.03
- parent_index: int32 [4096], P('dev'), may hold values from 0 to 255, as said below
- node_position: float32 [3, 6144], P(None, 'dev'), may hold values from -1 to 1
- node_angles: float32 [2, 6144], P(None, 'dev'), may hold values from -3.140625 to 3.140625
- block_receiver: int32 [4, 1024], P('grp', 'dev'), may hold values from 0 to 5
- block_source: int32 [4, 1024], P('grp', 'dev'), may hold values from 0 to 15
- block_count: int32 [4, 8], P('grp', 'dev'), may hold values from 16 to 128, as said below
Outputs:
- new_radiosity: float32 [3, 4096], P(None, 'dev')
Inputs may be any that keep to these rules, and one draw needn't show every extreme that they name: `parent_index`: within each shard's 512 leaves every cluster 0 to 255 is named at least once. The first block_count slots of a device are live, the rest are ignored. For every index of dev exactly one index of grp has 128 live slots; the others have at most 64.
All inputs are finite; a program needn't handle non-finite values.
Results may differ from a plain program's by a relative error of at most 0.0001.
Values sent between devices are 32-bit elements; how exact they have to be, the bound alone decides.
A program may use at most 64 MiB of HBM per device.

v0:
```python
import functools
import jax
import jax.numpy as jnp
from jax import lax
from jax.experimental import pallas as pl
from jax.experimental.pallas import tpu as pltpu
from jax.sharding import PartitionSpec as P

TILE = 128


batch_slots = 16


def unit_normals(node_angles):
    azimuth = node_angles[0]
    elevation = node_angles[1]
    return jnp.stack(
        [
            jnp.cos(azimuth) * jnp.cos(elevation),
            jnp.sin(azimuth) * jnp.cos(elevation),
            jnp.sin(elevation),
        ]
    )


def tile_irradiance(receivers, sources):
    offsets = [
        sources[axis_id][:, None, :] - receivers[axis_id][:, :, None] for axis_id in range(3)
    ]
    distance_sq = offsets[0] * offsets[0] + offsets[1] * offsets[1] + offsets[2] * offsets[2]
    facing_receiver = (
        receivers[3][:, :, None] * offsets[0]
        + receivers[4][:, :, None] * offsets[1]
        + receivers[5][:, :, None] * offsets[2]
    )
    facing_source = (
        sources[3][:, None, :] * offsets[0]
        + sources[4][:, None, :] * offsets[1]
        + sources[5][:, None, :] * offsets[2]
    )
    source_area = sources[6][:, None, :]
    factor = (
        source_area
        * jnp.maximum(facing_receiver, 0.0)
        * jnp.maximum(-facing_source, 0.0)
        / ((distance_sq + source_area) * (jnp.pi * distance_sq + source_area))
    )
    return jnp.einsum("bij,cbj->bci", factor, sources[7:10], precision=lax.Precision.HIGHEST)


def listed_body(
    leaf_emit,
    leaf_albedo,
    leaf_radiosity,
    leaf_area,
    parent_index,
    node_position,
    node_angles,
    block_receiver,
    block_source,
    block_count,
):
    leaf_count = leaf_area.shape[0]
    node_count = node_position.shape[1]
    cluster_count = node_count - leaf_count
    tile_count = node_count // TILE
    slot_count = block_receiver.shape[1]
    normals = unit_normals(node_angles)
    parent_onehot = (
        parent_index[:, None] == jnp.arange(cluster_count, dtype=jnp.int32)[None, :]
    ).astype(jnp.float32)
    cluster_area = jnp.dot(leaf_area, parent_onehot, precision=lax.Precision.HIGHEST)
    weighted = jnp.dot(
        leaf_radiosity * leaf_area[None, :], parent_onehot, precision=lax.Precision.HIGHEST
    )
    cluster_radiosity = weighted / cluster_area[None, :]
    source_pack = jnp.concatenate(
        [
            node_position[:, leaf_count:],
            normals[:, leaf_count:],
            cluster_area[None, :],
            cluster_radiosity,
        ],
        axis=0,
    )
    receiver_pack = jnp.concatenate([node_position, normals], axis=0)
    linked = lax.all_to_all(receiver_pack, "dev", split_axis=1, concat_axis=1, tiled=True)
    receiver_tiles = linked.reshape(6, tile_count, TILE)
    everything = lax.all_gather(source_pack, "dev", axis=1, tiled=True)
    source_tiles = everything.reshape(10, -1, TILE)
    receiver_ids = block_receiver[0]
    source_ids = block_source[0]
    live_count = block_count[0, 0]
    step_slots = min(batch_slots, slot_count)

    def add_batch(rounds, totals):
        first = rounds * step_slots
        batch_receivers = lax.dynamic_slice_in_dim(receiver_ids, first, step_slots, 0)
        batch_sources = lax.dynamic_slice_in_dim(source_ids, first, step_slots, 0)
        batch_weight = (first + jnp.arange(step_slots, dtype=jnp.int32) < live_count).astype(
            jnp.float32
        )
        receivers = jnp.take(receiver_tiles, batch_receivers, axis=1)
        sources = jnp.take(source_tiles, batch_sources, axis=1)
        contrib = tile_irradiance(receivers, sources) * batch_weight[:, None, None]
        placement = (
            batch_receivers[:, None] == jnp.arange(tile_count, dtype=jnp.int32)[None, :]
        ).astype(jnp.float32)
        return totals + jnp.einsum(
            "bt,bci->cti", placement, contrib, precision=lax.Precision.HIGHEST
        )

    batch_total = (live_count + step_slots - 1) // step_slots
    totals = lax.fori_loop(0, batch_total, add_batch, jnp.zeros((3, tile_count, TILE), jnp.float32))
    partial_value = totals.reshape(3, node_count)
    summed = lax.psum(partial_value, "grp")
    irradiance = lax.all_to_all(summed, "dev", split_axis=1, concat_axis=1, tiled=True)
    pushed = jnp.dot(irradiance[:, leaf_count:], parent_onehot.T, precision=lax.Precision.HIGHEST)
    gathered = irradiance[:, :leaf_count] + pushed
    return leaf_emit + leaf_albedo * gathered


F32 = jnp.float32
BF16 = jnp.bfloat16
MESH = pl.DeviceIdType.MESH
ROWS = 10
NT_DIMS = (((1,), (1,)), ((), ()))


def split3(values):
    high = values.astype(BF16)
    rest = values - high.astype(F32)
    middle = rest.astype(BF16)
    low = (rest - middle.astype(F32)).astype(BF16)
    return [high.astype(F32), middle.astype(F32), low.astype(F32)]


def stack3(values):
    rows = values.shape[0]
    pad = jnp.zeros((16 - 3 * rows, values.shape[1]), F32)
    return jnp.concatenate(split3(values) + [pad], axis=0).astype(BF16)


def unstack3(product, rows):
    return product[0:rows] + product[rows : 2 * rows] + product[2 * rows : 3 * rows]


def dense_kernel(
    groups, shards, *refs
):
    operands, out, inputs, scratch = refs[:8], refs[8], refs[9:17], refs[17:]
    radiosity, area, parent, position, angles, receiver_id, source_id, count = inputs
    (
        packs, sources, columns, my_hist, hists, receivers, onehot, place, sums, part, gathered,
        load, src_send, src_recv, hist_send, hist_recv, part_send, part_recv,
    ) = scratch
    g = lax.axis_index("grp")
    k = lax.axis_index("dev")
    device_total = groups * shards
    me = g * shards + k
    leaves = radiosity.shape[1]
    nodes = position.shape[1]
    clusters = nodes - leaves
    per_shard = clusters // TILE
    source_tiles = shards * per_shard
    tiles_here = source_tiles // groups
    per_peer = nodes // shards
    chunks = nodes // TILE

    barrier = pltpu.get_barrier_semaphore()

    far_first = sorted(range(shards), key=lambda step: -min(step, shards - step))
    others = [
        ((g + group_step) % groups, (k + step) % shards)
        for step in far_first
        for group_step in reversed(range(groups))
        if group_step or step
    ]
    for other in others:
        pl.semaphore_signal(barrier, inc=1, device_id=other, device_id_type=MESH)
    loads = [
        pltpu.make_async_copy(operands[i], inputs[i], load.at[i]) for i in range(len(inputs))
    ]
    for copy in loads:
        copy.start()
    for copy in loads:
        copy.wait()

    lane = lax.broadcasted_iota(jnp.int32, (1, TILE), 1)
    code = receiver_id[...] * source_tiles + source_id[...]
    code = jnp.where(lane < jnp.broadcast_to(count[...], (1, TILE)), code, -1)
    square = lax.broadcasted_iota(jnp.int32, (TILE, TILE), 0)
    hit = jnp.where(square == code, 1.0, 0.0).astype(BF16)
    counted = lax.dot_general(
        jnp.ones((16, TILE), BF16), hit, NT_DIMS, preferred_element_type=F32
    )
    my_hist[...] = counted[0:1]
    hists[me] = counted[0:1]

    ids = lax.broadcasted_iota(jnp.int32, (clusters, leaves), 0)
    onehot[...] = jnp.where(ids == parent[...], 1.0, 0.0).astype(BF16)
    area_row = area[...]
    stacked = stack3(jnp.concatenate([area_row, radiosity[...] * area_row], axis=0))
    cluster = unstack3(
        lax.dot_general(stacked, onehot[...], NT_DIMS, preferred_element_type=F32), 4
    )
    cosines = jnp.cos(angles[...])
    sines = jnp.sin(angles[...])
    normals = [cosines[0:1] * cosines[1:2], sines[0:1] * cosines[1:2], sines[1:2]]
    node_rows = [position[i : i + 1, :] for i in range(3)] + normals
    for half in range(per_shard):
        first = leaves + half * TILE
        rows = [row[:, first : first + TILE] for row in node_rows]
        rows.append(cluster[:, half * TILE : (half + 1) * TILE])
        packs[half] = jnp.concatenate(rows, axis=0)

    half = (g + groups * shards * per_shard - per_shard * k) % groups
    is_owner = half < per_shard
    mine = (per_shard * k + half) // groups

    pl.semaphore_wait(barrier, device_total - 1)

    def source_copy(step):
        return pltpu.make_async_remote_copy(
            src_ref=packs.at[half],
            dst_ref=sources.at[mine],
            send_sem=src_send.at[step - 1],
            recv_sem=src_recv.at[mine],
            device_id=(g, (k + step) % shards),
            device_id_type=MESH,
        )

    @pl.when(is_owner)
    def _():
        for step in range(1, shards):
            source_copy(step).start()
        sources[mine] = packs[half]

    for other in others:
        pltpu.make_async_remote_copy(
            src_ref=my_hist,
            dst_ref=hists.at[me],
            send_sem=hist_send,
            recv_sem=hist_recv,
            device_id=other,
            device_id_type=MESH,
        ).start()

    for i in range(6):
        receivers[i] = jnp.broadcast_to(node_rows[i], (8, nodes))
    tile_slots = TILE // source_tiles
    node = lax.broadcasted_iota(jnp.int32, (1, nodes), 1)
    link = jnp.zeros((1, nodes), jnp.int32)
    for j in range(1, shards):
        link += jnp.where(node >= j * per_peer, 1, 0)
    spot = k * per_peer + node - link * per_peer
    tile_of = jnp.zeros((1, nodes), jnp.int32)
    for t in range(1, chunks):
        tile_of += jnp.where(spot >= t * TILE, 1, 0)
    node_key = tile_of * shards + link
    where_rows = []
    for t in range(tile_slots):
        row = lax.broadcasted_iota(jnp.int32, (device_total, nodes), 0)
        key = t * shards + row % shards
        where_rows.append(jnp.where(key == node_key, 1.0, 0.0))
    place[...] = jnp.concatenate(where_rows, axis=0).astype(BF16)

    nearest = per_shard * k // groups
    for turn in range(tiles_here):
        m = (nearest + turn) % tiles_here
        owner = (groups * m + g) // per_shard

        @pl.when(k != owner)
        def _():
            pltpu.make_async_remote_copy(
                src_ref=packs.at[0],
                dst_ref=sources.at[m],
                send_sem=src_send.at[0],
                recv_sem=src_recv.at[m],
                device_id=(g, owner),
                device_id_type=MESH,
            ).wait_recv()

        padded = jnp.concatenate([sources[m], jnp.zeros((16 - ROWS, TILE), F32)], axis=0)
        columns[...] = jnp.transpose(padded)

        def add_sources(step, totals):
            block = columns[pl.ds(pl.multiple_of(step * 8, 8), 8), :]
            y0, y1, y2, m0, m1, m2, a, w0, w1, w2 = [
                jnp.broadcast_to(block[:, i : i + 1], (8, TILE)) for i in range(ROWS)
            ]
            result = []
            for chunk in range(chunks):
                x0, x1, x2, n0, n1, n2 = [
                    receivers[i, :, chunk * TILE : (chunk + 1) * TILE] for i in range(6)
                ]
                d0, d1, d2 = y0 - x0, y1 - x1, y2 - x2
                r2 = d0 * d0 + d1 * d1 + d2 * d2
                toward = jnp.maximum(n0 * d0 + n1 * d1 + n2 * d2, 0.0)
                facing = jnp.minimum(m0 * d0 + m1 * d1 + m2 * d2, 0.0)
                form = toward * facing / ((r2 + a) * (jnp.pi * r2 + a))
                old = totals[3 * chunk : 3 * chunk + 3]
                result += [old[0] - form * w0, old[1] - form * w1, old[2] - form * w2]
            return tuple(result)

        zero = jnp.zeros((8, TILE), F32)
        totals = lax.fori_loop(0, TILE // 8, add_sources, (zero,) * (3 * chunks), unroll=8)
        for chunk in range(chunks):
            for c in range(3):
                sums[3 * turn + c : 3 * turn + c + 1, chunk * TILE : (chunk + 1) * TILE] = jnp.sum(
                    totals[3 * chunk + c], axis=0, keepdims=True
                )

    all_but_one = hists.at[pl.ds(0, device_total - 1)]
    pltpu.make_async_copy(all_but_one, all_but_one, hist_recv).wait()
    table = jnp.concatenate([hists[d] for d in range(device_total)], axis=0)
    lanes = lax.broadcasted_iota(jnp.int32, (device_total, TILE), 1)
    by_tile = jnp.concatenate(
        [
            jnp.where((lanes >= t * source_tiles) & (lanes < (t + 1) * source_tiles), table, 0.0)
            for t in range(tile_slots)
        ],
        axis=0,
    ).astype(BF16)
    pick_row = lax.broadcasted_iota(jnp.int32, (16, TILE), 0)
    pick_lane = lax.broadcasted_iota(jnp.int32, (16, TILE), 1)
    pick = (pick_lane % source_tiles == groups * ((nearest + pick_row) % tiles_here) + g) & (pick_row < tiles_here)
    picked = lax.dot_general(
        jnp.where(pick, 1.0, 0.0).astype(BF16), by_tile, NT_DIMS, preferred_element_type=F32
    )
    weight = jnp.dot(picked.astype(BF16), place[...], preferred_element_type=F32)

    irradiance = weight[0:1] * sums[0:3, :]
    for m in range(1, tiles_here):
        irradiance += weight[m : m + 1] * sums[3 * m : 3 * m + 3, :]
    pushed = unstack3(
        jnp.dot(stack3(irradiance[:, leaves:]), onehot[...], preferred_element_type=F32), 3
    )
    part[...] = irradiance[:, :leaves] + pushed
    gathered[g] = irradiance[:, :leaves] + pushed

    def part_copy(step):
        return pltpu.make_async_remote_copy(
            src_ref=part,
            dst_ref=gathered.at[g],
            send_sem=part_send.at[step],
            recv_sem=part_recv.at[g],
            device_id=((g + step) % groups, k),
            device_id_type=MESH,
        )

    for step in range(1, groups):
        part_copy(step).start()
    for step in range(1, groups):
        sender = (g + step) % groups
        pltpu.make_async_remote_copy(
            src_ref=part,
            dst_ref=gathered.at[sender],
            send_sem=part_send.at[step],
            recv_sem=part_recv.at[sender],
            device_id=(sender, k),
            device_id_type=MESH,
        ).wait_recv()
    total = gathered[0]
    for other in range(1, groups):
        total += gathered[other]
    out[...] = total
    for step in range(1, groups):
        part_copy(step).wait_send()
    pltpu.make_async_copy(all_but_one, all_but_one, hist_send).wait()

    @pl.when(is_owner)
    def _():
        for step in range(1, shards):
            source_copy(step).wait_send()


def dense_body(
    groups, shards, leaf_emit, leaf_albedo, leaf_radiosity, leaf_area, parent_index,
    node_position, node_angles, block_receiver, block_source, block_count,
):
    leaves = leaf_area.shape[0]
    nodes = node_position.shape[1]
    clusters = nodes - leaves
    tiles_here = shards * clusters // TILE // groups
    operands = (
        leaf_radiosity, leaf_area[None, :], parent_index[None, :], node_position, node_angles,
        block_receiver, block_source, block_count,
    )
    gathered = pl.pallas_call(
        functools.partial(dense_kernel, groups, shards),
        out_shape=pltpu.VMEM((3, leaves), F32),
        in_specs=[pl.BlockSpec(memory_space=pl.ANY)] * len(operands),
        out_specs=pl.BlockSpec(memory_space=pltpu.VMEM),
        scratch_shapes=[pltpu.VMEM(x.shape, x.dtype) for x in operands]
        + [
            pltpu.VMEM((clusters // TILE, ROWS, TILE), F32),
            pltpu.VMEM((tiles_here, ROWS, TILE), F32),
            pltpu.VMEM((TILE, 16), F32),
            pltpu.VMEM((1, TILE), F32),
            pltpu.VMEM((groups * shards, 1, TILE), F32),
            pltpu.VMEM((6, 8, nodes), F32),
            pltpu.VMEM((clusters, leaves), BF16),
            pltpu.VMEM((TILE // (shards * clusters // TILE) * groups * shards, nodes), BF16),
            pltpu.VMEM((3 * tiles_here, nodes), F32),
            pltpu.VMEM((3, leaves), F32),
            pltpu.VMEM((groups, 3, leaves), F32),
            pltpu.SemaphoreType.DMA((len(operands),)),
            pltpu.SemaphoreType.DMA((shards - 1,)),
            pltpu.SemaphoreType.DMA((tiles_here,)),
            pltpu.SemaphoreType.DMA,
            pltpu.SemaphoreType.DMA,
            pltpu.SemaphoreType.DMA((groups,)),
            pltpu.SemaphoreType.DMA((groups,)),
        ],
        compiler_params=pltpu.CompilerParams(collective_id=0, has_side_effects=True),
    )(*operands)
    return leaf_emit + leaf_albedo * gathered


def body(groups, shards, *args):
    leaves, nodes, slots = args[3].shape[0], args[5].shape[1], args[7].shape[1]
    per_shard = (nodes - leaves) // TILE
    source_tiles = shards * per_shard
    dense = (
        nodes // TILE * source_tiles <= TILE
        and TILE % source_tiles == 0
        and source_tiles % groups == 0
        and per_shard <= groups
        and slots == TILE
    )
    return dense_body(groups, shards, *args) if dense else listed_body(*args)


def solution(mesh):
    in_specs = (
        P(None, "dev"),
        P(None, "dev"),
        P(None, "dev"),
        P("dev"),
        P("dev"),
        P(None, "dev"),
        P(None, "dev"),
        P("grp", "dev"),
        P("grp", "dev"),
        P("grp", "dev"),
    )
    out_specs = P(None, "dev")
    sized = functools.partial(body, mesh.shape["grp"], mesh.shape["dev"])
    return jax.shard_map(sized, mesh=mesh, in_specs=in_specs, out_specs=out_specs, check_vma=False)
```

profile of v0, /device:TPU:0, one launch (start us, length us, event | category | flops | bytes accessed | tf_op | source)
XLA Modules:
  0.0 15.8 jit_solution(3368954160864651533)
XLA Ops:
  0.7 0.0 copy-start
  0.7 0.0 copy-start.1
  0.7 14.5 %shard_map.100 = f32[3,512]{1,0:T(4,128)S(1)} custom-call(f32[3,512]{1,0:T(4,128)} %refs_0_.1, f32[1,512]{1,0:T(1,128)} %bitcast.2, s32[1,512]{1,0:T(1,128)} %bitcast.3, f32[3,768]{1,0:T(4,128)} %refs_3_.1, f32[2,768]{1,0:T(2,128)} %refs_4_.1, s32[1,128]{1,0:T(1,128)} %refs_5_.1, s32[1,128]{1,0:T(1,128)} %refs_6_.1, s32[1,1]{1,0:T(1,128)S(6)} %copy.11.refs_7_), custom_call_target="tpu_custom_call" | custom-call | tf_op jit(solution)/shard_map/pallas_call | solution.py:391
  15.2 0.0 copy-done
  15.2 0.0 copy-done.1
  15.2 0.6 %multiply_add_fusion = f32[3,512]{1,0:T(4,128)} fusion(f32[3,512]{1,0:T(4,128)S(1)} %copy-done, f32[3,512]{1,0:T(4,128)S(1)} %copy-done.1, f32[3,512]{1,0:T(4,128)S(1)} %shard_map.100), kind=kLoop, calls=%fused_computation | loop fusion | flops 3072 | bytes 24576 | tf_op jit(solution)/shard_map/add | solution.py:419
Async XLA Ops:
  0.7 14.6 %copy-start = (f32[3,512]{1,0:T(4,128)S(1)}, f32[3,512]{1,0:T(4,128)}, u32[]{:S(2)}) copy-start(f32[3,512]{1,0:T(4,128)} %param.10) | copy-start | bytes 18436
  0.7 14.6 %copy-start.1 = (f32[3,512]{1,0:T(4,128)S(1)}, f32[3,512]{1,0:T(4,128)}, u32[]{:S(2)}) copy-start(f32[3,512]{1,0:T(4,128)} %param.11) | copy-start | bytes 18436
where the time goes:
time: 16 us; the launch traced here: 15.8 us
  Pallas kernels  14.5 us (91%)
  between operations  0.69 us (4%)
  other arithmetic  0.6 us (4%)
    pallas_call x1, Pallas kernels, dense_body(): pl.pallas_call(functools.partial(dense_kernel, groups, shards), out_shape...  14.5 us
    add x1, other arithmetic, dense_body(): return leaf_emit + leaf_albedo * gathered  0.6 us

commit v1 on v0

v1 whole, which is shorter than its diff:
```python
import functools
import jax
import jax.numpy as jnp
from jax import lax
from jax.experimental import pallas as pl
from jax.experimental.pallas import tpu as pltpu
from jax.sharding import PartitionSpec as P

TILE = 128


batch_slots = 16


def unit_normals(node_angles):
    azimuth = node_angles[0]
    elevation = node_angles[1]
    return jnp.stack(
        [
            jnp.cos(azimuth) * jnp.cos(elevation),
            jnp.sin(azimuth) * jnp.cos(elevation),
            jnp.sin(elevation),
        ]
    )


def tile_irradiance(receivers, sources):
    offsets = [
        sources[axis_id][:, None, :] - receivers[axis_id][:, :, None] for axis_id in range(3)
    ]
    distance_sq = offsets[0] * offsets[0] + offsets[1] * offsets[1] + offsets[2] * offsets[2]
    facing_receiver = (
        receivers[3][:, :, None] * offsets[0]
        + receivers[4][:, :, None] * offsets[1]
        + receivers[5][:, :, None] * offsets[2]
    )
    facing_source = (
        sources[3][:, None, :] * offsets[0]
        + sources[4][:, None, :] * offsets[1]
        + sources[5][:, None, :] * offsets[2]
    )
    source_area = sources[6][:, None, :]
    factor = (
        source_area
        * jnp.maximum(facing_receiver, 0.0)
        * jnp.maximum(-facing_source, 0.0)
        / ((distance_sq + source_area) * (jnp.pi * distance_sq + source_area))
    )
    return jnp.einsum("bij,cbj->bci", factor, sources[7:10], precision=lax.Precision.HIGHEST)


def listed_body(
    leaf_emit,
    leaf_albedo,
    leaf_radiosity,
    leaf_area,
    parent_index,
    node_position,
    node_angles,
    block_receiver,
    block_source,
    block_count,
):
    leaf_count = leaf_area.shape[0]
    node_count = node_position.shape[1]
    cluster_count = node_count - leaf_count
    tile_count = node_count // TILE
    slot_count = block_receiver.shape[1]
    normals = unit_normals(node_angles)
    parent_onehot = (
        parent_index[:, None] == jnp.arange(cluster_count, dtype=jnp.int32)[None, :]
    ).astype(jnp.float32)
    cluster_area = jnp.dot(leaf_area, parent_onehot, precision=lax.Precision.HIGHEST)
    weighted = jnp.dot(
        leaf_radiosity * leaf_area[None, :], parent_onehot, precision=lax.Precision.HIGHEST
    )
    cluster_radiosity = weighted / cluster_area[None, :]
    source_pack = jnp.concatenate(
        [
            node_position[:, leaf_count:],
            normals[:, leaf_count:],
            cluster_area[None, :],
            cluster_radiosity,
        ],
        axis=0,
    )
    receiver_pack = jnp.concatenate([node_position, normals], axis=0)
    linked = lax.all_to_all(receiver_pack, "dev", split_axis=1, concat_axis=1, tiled=True)
    receiver_tiles = linked.reshape(6, tile_count, TILE)
    everything = lax.all_gather(source_pack, "dev", axis=1, tiled=True)
    source_tiles = everything.reshape(10, -1, TILE)
    receiver_ids = block_receiver[0]
    source_ids = block_source[0]
    live_count = block_count[0, 0]
    step_slots = min(batch_slots, slot_count)

    def add_batch(rounds, totals):
        first = rounds * step_slots
        batch_receivers = lax.dynamic_slice_in_dim(receiver_ids, first, step_slots, 0)
        batch_sources = lax.dynamic_slice_in_dim(source_ids, first, step_slots, 0)
        batch_weight = (first + jnp.arange(step_slots, dtype=jnp.int32) < live_count).astype(
            jnp.float32
        )
        receivers = jnp.take(receiver_tiles, batch_receivers, axis=1)
        sources = jnp.take(source_tiles, batch_sources, axis=1)
        contrib = tile_irradiance(receivers, sources) * batch_weight[:, None, None]
        placement = (
            batch_receivers[:, None] == jnp.arange(tile_count, dtype=jnp.int32)[None, :]
        ).astype(jnp.float32)
        return totals + jnp.einsum(
            "bt,bci->cti", placement, contrib, precision=lax.Precision.HIGHEST
        )

    batch_total = (live_count + step_slots - 1) // step_slots
    totals = lax.fori_loop(0, batch_total, add_batch, jnp.zeros((3, tile_count, TILE), jnp.float32))
    partial_value = totals.reshape(3, node_count)
    summed = lax.psum(partial_value, "grp")
    irradiance = lax.all_to_all(summed, "dev", split_axis=1, concat_axis=1, tiled=True)
    pushed = jnp.dot(irradiance[:, leaf_count:], parent_onehot.T, precision=lax.Precision.HIGHEST)
    gathered = irradiance[:, :leaf_count] + pushed
    return leaf_emit + leaf_albedo * gathered


F32 = jnp.float32
BF16 = jnp.bfloat16
MESH = pl.DeviceIdType.MESH
NT_DIMS = (((1,), (1,)), ((), ()))
FEATURES = 8
ROWS = 64


def split3(values):
    high = values.astype(BF16).astype(F32)
    rest = values - high
    middle = rest.astype(BF16).astype(F32)
    return high, middle, rest - middle


def stack3(values):
    rows = values.shape[0]
    pad = jnp.zeros((16 - 3 * rows, values.shape[1]), F32)
    return jnp.concatenate(list(split3(values)) + [pad], axis=0).astype(BF16)


def unstack3(product, rows):
    return product[0:rows] + product[rows : 2 * rows] + product[2 * rows : 3 * rows]


def flip(k, turn, shards):
    value, bit = 0, 1
    while bit < shards:
        digit = k // bit % 2
        value = value + bit * ((1 - digit) if turn // bit % 2 else digit)
        bit *= 2
    return value


def paired_rows(left, const):
    one, two, three = split3(left)
    row = lax.broadcasted_iota(jnp.int32, left.shape, 0)
    free = (row == 6) | (row == 7)
    plain = [jnp.where(free, 0.0, part) for part in (one, two, three)]
    zero = jnp.zeros_like(left)
    c1, c2, c3 = [zero] * 3 if const is None else split3(jnp.broadcast_to(const, left.shape))
    at6 = row == 6
    with_sum = jnp.where(free, left, one)
    return jnp.concatenate(
        [
            with_sum,
            jnp.where(at6, c1, plain[1]),
            jnp.where(at6, c2, plain[2]),
            with_sum,
            jnp.where(at6, c3, plain[1]),
            with_sum,
        ],
        axis=0,
    ).astype(BF16)


def dense_kernel(groups, shards, *refs):
    operands, count, out, inputs, scratch = refs[:7], refs[7], refs[8], refs[9:16], refs[16:]
    receiver_id, source_id, radiosity, area, parent, position, angles = inputs
    (
        load,
        sources, my_pack, my_hist, hists, right, onehot, place, columns, turned, sums,
        src_send, src_recv, hist_send, hist_recv,
    ) = scratch
    g = lax.axis_index("grp")
    k = lax.axis_index("dev")
    device_total = groups * shards
    me = g * shards + k
    leaves = radiosity.shape[1]
    nodes = position.shape[1]
    clusters = nodes - leaves
    per_shard = clusters // TILE
    source_tiles = shards * per_shard
    per_peer = nodes // shards
    chunks = nodes // TILE
    pairs = nodes // (2 * TILE)

    loads = [
        pltpu.make_async_copy(operands[i], inputs[i], load.at[i]) for i in range(len(inputs))
    ]
    for copy in loads:
        copy.start()

    barrier = pltpu.get_barrier_semaphore()
    far_first = sorted(range(shards), key=lambda step: -step)
    others = [
        ((g + group_step) % groups, flip(k, step, shards))
        for step in far_first
        for group_step in reversed(range(groups))
        if group_step or step
    ]
    for other in others:
        pl.semaphore_signal(barrier, inc=1, device_id=other, device_id_type=MESH)

    for copy in loads:
        copy.wait()

    lane = lax.broadcasted_iota(jnp.int32, (1, TILE), 1)
    code = jnp.where(
        lane < count[0, 0], receiver_id[...] * source_tiles + source_id[...], -1
    )
    square = lax.broadcasted_iota(jnp.int32, (TILE, TILE), 0)
    hit = jnp.where(square == code, 1.0, 0.0).astype(BF16)
    counted = lax.dot_general(
        jnp.ones((16, TILE), BF16), hit, NT_DIMS, preferred_element_type=F32
    )
    my_hist[...] = counted[0:1]
    hists[me] = counted[0:1]

    ids = lax.broadcasted_iota(jnp.int32, (clusters, leaves), 0)
    onehot[...] = jnp.where(ids == parent[...], 1.0, 0.0).astype(BF16)
    area_row = area[...]
    stacked = stack3(jnp.concatenate([area_row, radiosity[...] * area_row], axis=0))
    cluster = unstack3(
        lax.dot_general(stacked, onehot[...], NT_DIMS, preferred_element_type=F32), 4
    )
    cosines = jnp.cos(angles[...])
    sines = jnp.sin(angles[...])
    normals = jnp.concatenate(
        [cosines[0:1] * cosines[1:2], sines[0:1] * cosines[1:2], sines[1:2]], axis=0
    )
    first_band = cluster[1:2] * (1.0 / jnp.pi)
    facing = normals[:, leaves:] * first_band
    ratios = cluster[2:4] / cluster[1:2]
    for half in range(per_shard):
        here = slice(half * TILE, (half + 1) * TILE)
        there = slice(leaves + half * TILE, leaves + (half + 1) * TILE)
        my_pack[8 * half : 8 * half + 8, :] = jnp.concatenate(
            [position[:, there], facing[:, here], cluster[0:1, here], ratios[0:1, here]], axis=0
        )
        my_pack[8 * per_shard + half : 8 * per_shard + half + 1, :] = ratios[1:2, here]

    pl.semaphore_wait(barrier, device_total - 1)

    for other in others:
        pltpu.make_async_remote_copy(
            src_ref=my_hist,
            dst_ref=hists.at[me],
            send_sem=hist_send,
            recv_sem=hist_recv,
            device_id=other,
            device_id_type=MESH,
        ).start()

    def source_copy(step):
        return pltpu.make_async_remote_copy(
            src_ref=my_pack,
            dst_ref=sources.at[k],
            send_sem=src_send.at[step - 1],
            recv_sem=src_recv.at[k],
            device_id=(g, flip(k, step, shards)),
            device_id_type=MESH,
        )

    for step in far_first:
        if step:
            source_copy(step).start()

    middle = jnp.sum(position[...], axis=1, keepdims=True) * (1.0 / nodes)
    centred = position[...] - middle
    ones = jnp.ones((1, nodes), F32)
    none = jnp.zeros((1, nodes), F32)
    three = jnp.zeros((3, nodes), F32)
    offset = -jnp.sum(normals * centred, axis=0, keepdims=True)
    norm = jnp.sum(centred * centred, axis=0, keepdims=True)
    for which, rows in enumerate(
        (
            paired_rows(jnp.concatenate([normals, three, none, none], axis=0), offset),
            paired_rows(jnp.concatenate([three, centred, -ones, none], axis=0), None),
            paired_rows(jnp.concatenate([-2.0 * centred, three, none, ones], axis=0), norm),
        )
    ):
        right[which] = rows

    node = lax.broadcasted_iota(jnp.int32, (1, nodes), 1)
    link = jnp.zeros((1, nodes), jnp.int32)
    for j in range(1, shards):
        link += jnp.where(node >= j * per_peer, 1, 0)
    spot = k * per_peer + node - link * per_peer
    low_tile = k * per_peer // TILE
    high_tile = (k * per_peer + per_peer - 1) // TILE
    upper = spot >= (low_tile + 1) * TILE
    owner_row = lax.broadcasted_iota(jnp.int32, (device_total, nodes), 0) % shards
    hits = owner_row == link
    place[0] = jnp.where(hits & ~upper, 1.0, 0.0).astype(BF16)
    place[1] = jnp.where(hits & upper, 1.0, 0.0).astype(BF16)

    row8 = lax.broadcasted_iota(jnp.int32, (8, TILE), 0)
    centre8 = jnp.concatenate([middle, jnp.zeros((5, 1), F32)], axis=0)

    def tile_sums(pack, half, tile):
        values = pack[8 * half : 8 * half + 8, :]
        ratio = pack[8 * per_shard + half : 8 * per_shard + half + 1, :]
        area_here = values[6:7]
        shifted = values - centre8
        spots, aims = shifted[0:3], shifted[3:6]
        along = jnp.sum(spots * aims, axis=0, keepdims=True)
        reach = jnp.sum(spots * spots, axis=0, keepdims=True) + area_here
        one, two, low = split3(jnp.concatenate([spots, aims, along, reach], axis=0))
        left = jnp.concatenate(
            [
                one,
                jnp.where(row8 == 6, 1.0, one),
                jnp.where(row8 == 6, 1.0, one),
                two,
                jnp.where(row8 == 6, 1.0, two),
                low,
            ],
            axis=0,
        )
        extra = jnp.concatenate(
            [values[7:8], ratio, area_here * ((jnp.pi - 1.0) / jnp.pi), jnp.zeros((5, TILE), F32)],
            axis=0,
        )
        features = jnp.transpose(left).astype(BF16)
        column = jnp.transpose(extra)
        second, third, less = [
            jnp.broadcast_to(column[:, i : i + 1], (TILE, TILE)) for i in range(3)
        ]
        for pair in range(pairs):
            wide = slice(pair * 2 * TILE, (pair + 1) * 2 * TILE)
            totals = [[None] * 3, [None] * 3]
            for first in range(0, TILE, ROWS):
                some = slice(first, first + ROWS)
                toward, facing, span = [
                    jnp.dot(features[some], right[which, :, wide], preferred_element_type=F32)
                    for which in range(3)
                ]
                for side in range(2):
                    lanes = slice(side * TILE, (side + 1) * TILE)
                    u = span[:, lanes]
                    form = (
                        jnp.maximum(toward[:, lanes], 0.0)
                        * jnp.maximum(facing[:, lanes], 0.0)
                        / (u * (u - less[some]))
                    )
                    for c, scaled in enumerate((form, form * second[some], form * third[some])):
                        part = jnp.sum(scaled.reshape(ROWS // 8, 8, TILE), axis=0)
                        old = totals[side][c]
                        totals[side][c] = part if old is None else old + part
            for side in range(2):
                first = pair * 2 * TILE + side * TILE
                for c in range(3):
                    sums[tile, c : c + 1, first : first + TILE] = jnp.sum(
                        totals[side][c], axis=0, keepdims=True
                    )

    for first in range(0, shards, 2):
        packs = []
        for turn in (first, first + 1):
            owner = flip(k, turn, shards)
            if turn:
                pltpu.make_async_remote_copy(
                    src_ref=my_pack,
                    dst_ref=sources.at[owner],
                    send_sem=src_send.at[0],
                    recv_sem=src_recv.at[owner],
                    device_id=(g, owner),
                    device_id_type=MESH,
                ).wait_recv()
            packs.append((sources.at[owner] if turn else my_pack, owner))
        for pack, owner in packs:
            for half in range(per_shard):
                tile_sums(pack, half, owner * per_shard + half)

    all_but_one = hists.at[pl.ds(0, device_total - 1)]
    pltpu.make_async_copy(all_but_one, all_but_one, hist_recv).wait()
    table = jnp.concatenate([hists[d] for d in range(device_total)], axis=0)
    turned[...] = jnp.transpose(table)
    weight = jnp.zeros((source_tiles, nodes), F32)
    for which, tile in enumerate((low_tile, high_tile)):
        rows = turned[pl.ds(pl.multiple_of(tile * source_tiles, 8), source_tiles), :]
        weight += jnp.dot(rows.astype(BF16), place[which], preferred_element_type=F32)

    irradiance = weight[0:1] * sums[0]
    for tile in range(1, source_tiles):
        irradiance += weight[tile : tile + 1] * sums[tile]
    pushed = unstack3(
        jnp.dot(stack3(irradiance[:, leaves:]), onehot[...], preferred_element_type=F32), 3
    )
    out[...] = irradiance[:, :leaves] + pushed

    pltpu.make_async_copy(all_but_one, all_but_one, hist_send).wait()
    for step in far_first:
        if step:
            source_copy(step).wait_send()


def dense_body(
    groups, shards, leaf_emit, leaf_albedo, leaf_radiosity, leaf_area, parent_index,
    node_position, node_angles, block_receiver, block_source, block_count,
):
    leaves = leaf_area.shape[0]
    nodes = node_position.shape[1]
    clusters = nodes - leaves
    per_shard = clusters // TILE
    source_tiles = shards * per_shard
    device_total = groups * shards
    operands = (
        block_receiver, block_source, leaf_radiosity, leaf_area[None, :], parent_index[None, :],
        node_position, node_angles,
    )
    pack_rows = 9 * per_shard
    gathered = pl.pallas_call(
        functools.partial(dense_kernel, groups, shards),
        out_shape=pltpu.VMEM((3, leaves), F32),
        in_specs=[pl.BlockSpec(memory_space=pltpu.HBM)] * len(operands)
        + [pl.BlockSpec(memory_space=pltpu.SMEM)],
        out_specs=pl.BlockSpec(memory_space=pltpu.VMEM),
        scratch_shapes=[pltpu.VMEM(x.shape, x.dtype) for x in operands]
        + [
            pltpu.SemaphoreType.DMA((len(operands),)),
            pltpu.VMEM((shards, pack_rows, TILE), F32),
            pltpu.VMEM((pack_rows, TILE), F32),
            pltpu.VMEM((1, TILE), F32),
            pltpu.VMEM((device_total, 1, TILE), F32),
            pltpu.VMEM((3, 6 * FEATURES, nodes), BF16),
            pltpu.VMEM((clusters, leaves), BF16),
            pltpu.VMEM((2, device_total, nodes), BF16),
            pltpu.VMEM((TILE, TILE), F32),
            pltpu.VMEM((TILE, device_total), F32),
            pltpu.VMEM((source_tiles, 3, nodes), F32),
            pltpu.SemaphoreType.DMA((shards - 1,)),
            pltpu.SemaphoreType.DMA((shards,)),
            pltpu.SemaphoreType.DMA,
            pltpu.SemaphoreType.DMA,
        ],
        compiler_params=pltpu.CompilerParams(collective_id=0, has_side_effects=True),
    )(*operands, block_count)
    return leaf_emit + leaf_albedo * gathered


def body(groups, shards, *args):
    leaves, nodes, slots = args[3].shape[0], args[5].shape[1], args[7].shape[1]
    per_shard = (nodes - leaves) // TILE
    source_tiles = shards * per_shard
    dense = (
        nodes // TILE * source_tiles <= TILE
        and TILE % source_tiles == 0
        and source_tiles % 8 == 0
        and nodes % (2 * TILE) == 0
        and nodes % shards == 0
        and nodes // shards <= TILE
        and shards & (shards - 1) == 0
        and shards % 2 == 0
        and groups * shards <= TILE
        and slots == TILE
    )
    return dense_body(groups, shards, *args) if dense else listed_body(*args)


def solution(mesh):
    in_specs = (
        P(None, "dev"),
        P(None, "dev"),
        P(None, "dev"),
        P("dev"),
        P("dev"),
        P(None, "dev"),
        P(None, "dev"),
        P("grp", "dev"),
        P("grp", "dev"),
        P("grp", "dev"),
    )
    out_specs = P(None, "dev")
    sized = functools.partial(body, mesh.shape["grp"], mesh.shape["dev"])
    return jax.shard_map(sized, mesh=mesh, in_specs=in_specs, out_specs=out_specs, check_vma=False)
```

time: 16 us -> 15 us (0.938)
  Pallas kernels: 14.5 us -> 13.5 us
    pallas_call x1, Pallas kernels: 14.5 us -> 13.5 us  [dense_body(): pl.pallas_call(functools.partial(dense_kernel, groups, shards), out_shape...]
where the time goes in v1:
time: 15 us; the launch traced here: 14.8 us
  Pallas kernels  13.5 us (90%)
  between operations  0.69 us (5%)
  other arithmetic  0.6 us (4%)
    pallas_call x1, Pallas kernels, dense_body(): pl.pallas_call(functools.partial(dense_kernel, groups, shards), out_shape...  13.5 us
    add x1, other arithmetic, dense_body(): return leaf_emit + leaf_albedo * gathered  0.6 us

profile of v1, /device:TPU:0, one launch (start us, length us, event | category | flops | bytes accessed | tf_op | source)
XLA Modules:
  0.0 14.8 jit_solution(6137101101626435208)
XLA Ops:
  0.7 0.0 copy-start
  0.7 0.0 copy-start.1
  0.7 13.5 %shard_map.100 = f32[3,512]{1,0:T(4,128)S(1)} custom-call(s32[1,128]{1,0:T(1,128)} %refs_0_.1, s32[1,128]{1,0:T(1,128)} %refs_1_.1, f32[3,512]{1,0:T(4,128)} %refs_2_.1, f32[1,512]{1,0:T(1,128)} %bitcast.2, s32[1,512]{1,0:T(1,128)} %bitcast.3, f32[3,768]{1,0:T(4,128)} %refs_5_.1, f32[2,768]{1,0:T(2,128)} %refs_6_.1, s32[1,1]{1,0:T(1,128)S(6)} %copy.11.refs_7_), custom_call_target="tpu_custom_call" | custom-call | tf_op jit(solution)/shard_map/pallas_call | solution.py:427
  14.2 0.0 copy-done
  14.2 0.0 copy-done.1
  14.2 0.6 %multiply_add_fusion = f32[3,512]{1,0:T(4,128)} fusion(f32[3,512]{1,0:T(4,128)S(1)} %copy-done, f32[3,512]{1,0:T(4,128)S(1)} %copy-done.1, f32[3,512]{1,0:T(4,128)S(1)} %shard_map.100), kind=kLoop, calls=%fused_computation | loop fusion | flops 3072 | bytes 24576 | tf_op jit(solution)/shard_map/add | solution.py:453
Async XLA Ops:
  0.7 13.5 %copy-start = (f32[3,512]{1,0:T(4,128)S(1)}, f32[3,512]{1,0:T(4,128)}, u32[]{:S(2)}) copy-start(f32[3,512]{1,0:T(4,128)} %param.10) | copy-start | bytes 18436
  0.7 13.5 %copy-start.1 = (f32[3,512]{1,0:T(4,128)S(1)}, f32[3,512]{1,0:T(4,128)}, u32[]{:S(2)}) copy-start(f32[3,512]{1,0:T(4,128)} %param.11) | copy-start | bytes 18436

commit v2 on v1

--- a/solution.py
+++ b/solution.py
@@ -126,6 +126,7 @@
 MESH = pl.DeviceIdType.MESH
 NT_DIMS = (((1,), (1,)), ((), ()))
 FEATURES = 8
+RELAY_TURN = 4
 ROWS = 64
 
 
@@ -151,6 +152,16 @@
     while bit < shards:
         digit = k // bit % 2
         value = value + bit * ((1 - digit) if turn // bit % 2 else digit)
+        bit *= 2
+    return value
+
+
+def all_bits(g, pattern, groups, wanted):
+    value, bit = 1, 1
+    while bit < groups:
+        if pattern // bit % 2:
+            digit = g // bit % 2
+            value = value * (digit if wanted else 1 - digit)
         bit *= 2
     return value
 
@@ -183,7 +194,7 @@
     (
         load,
         sources, my_pack, my_hist, hists, right, onehot, place, columns, turned, sums,
-        src_send, src_recv, hist_send, hist_recv,
+        src_send, src_recv, hist_send, hist_recv, pass_send, peer_recv,
     ) = scratch
     g = lax.axis_index("grp")
     k = lax.axis_index("dev")
@@ -206,14 +217,24 @@
 
     barrier = pltpu.get_barrier_semaphore()
     far_first = sorted(range(shards), key=lambda step: -step)
-    others = [
-        ((g + group_step) % groups, flip(k, step, shards))
-        for step in far_first
-        for group_step in reversed(range(groups))
-        if group_step or step
-    ]
-    for other in others:
-        pl.semaphore_signal(barrier, inc=1, device_id=other, device_id_type=MESH)
+    group = [flip(g, e, groups) for e in range(groups)]
+    drops = [all_bits(g, e, groups, True) for e in range(groups)]
+    clear = [all_bits(g, e, groups, False) for e in range(groups)]
+
+    def greet(e, shard):
+        pl.semaphore_signal(
+            barrier, inc=1, device_id=(group[e], shard), device_id_type=MESH
+        )
+
+    for e in reversed(range(groups)):
+
+        @pl.when(clear[e] == 1)
+        def _():
+            lax.fori_loop(0, k, lambda shard, _: (greet(e, shard), 0)[1], 0)
+
+        lax.fori_loop(k + 1, shards, lambda shard, _: (greet(e, shard), 0)[1], 0)
+        if e:
+            greet(e, k)
 
     for copy in loads:
         copy.wait()
@@ -253,17 +274,38 @@
         )
         my_pack[8 * per_shard + half : 8 * per_shard + half + 1, :] = ratios[1:2, here]
 
-    pl.semaphore_wait(barrier, device_total - 1)
-
-    for other in others:
-        pltpu.make_async_remote_copy(
+    drop_total = sum(drops[1:], 1)
+    pl.semaphore_wait(barrier, groups - 1 + groups * k + (shards - 1 - k) * drop_total)
+
+    def hist_copy(e, shard):
+        return pltpu.make_async_remote_copy(
             src_ref=my_hist,
             dst_ref=hists.at[me],
-            send_sem=hist_send,
+            send_sem=hist_send.at[e * shards + shard],
             recv_sem=hist_recv,
-            device_id=other,
+            device_id=(group[e], shard),
             device_id_type=MESH,
-        ).start()
+        )
+
+    def peer_copy(e):
+        return pltpu.make_async_remote_copy(
+            src_ref=my_hist,
+            dst_ref=hists.at[me],
+            send_sem=hist_send.at[e * shards + k],
+            recv_sem=peer_recv.at[e],
+            device_id=(group[e], k),
+            device_id_type=MESH,
+        )
+
+    def passed_copy(e, shard):
+        return pltpu.make_async_remote_copy(
+            src_ref=hists.at[group[e] * shards + k],
+            dst_ref=hists.at[group[e] * shards + k],
+            send_sem=pass_send.at[e * shards + shard],
+            recv_sem=hist_recv,
+            device_id=(g, shard),
+            device_id_type=MESH,
+        )
 
     def source_copy(step):
         return pltpu.make_async_remote_copy(
@@ -275,9 +317,21 @@
             device_id_type=MESH,
         )
 
+    def run(first, last, action):
+        lax.fori_loop(first, last, lambda shard, _: (action(shard), 0)[1], 0)
+
+    for e in reversed(range(groups)):
+        run(0, k, lambda shard: hist_copy(e, shard).start())
     for step in far_first:
         if step:
             source_copy(step).start()
+    for e in range(1, groups):
+        peer_copy(e).start()
+    for e in range(groups):
+
+        @pl.when(drops[e] == 1)
+        def _():
+            run(k + 1, shards, lambda shard: hist_copy(e, shard).start())
 
     middle = jnp.sum(position[...], axis=1, keepdims=True) * (1.0 / nodes)
     centred = position[...] - middle
@@ -369,6 +423,39 @@
                     )
 
     for first in range(0, shards, 2):
+        if first == RELAY_TURN:
+            for e in range(1, groups):
+                pltpu.make_async_remote_copy(
+                    src_ref=my_hist,
+                    dst_ref=hists.at[group[e] * shards + k],
+                    send_sem=hist_send.at[0],
+                    recv_sem=peer_recv.at[e],
+                    device_id=(group[e], k),
+                    device_id_type=MESH,
+                ).wait_recv()
+
+                @pl.when(clear[e] == 0)
+                def _():
+                    run(k + 1, shards, lambda shard: passed_copy(e, shard).start())
+
+        if first == shards - 2:
+            for e in range(groups):
+                run(0, k, lambda shard: hist_copy(e, shard).wait_send())
+
+                @pl.when(drops[e] == 1)
+                def _():
+                    run(k + 1, shards, lambda shard: hist_copy(e, shard).wait_send())
+
+                if e:
+                    peer_copy(e).wait_send()
+
+                    @pl.when(clear[e] == 0)
+                    def _():
+                        run(k + 1, shards, lambda shard: passed_copy(e, shard).wait_send())
+
+            for step in far_first:
+                if step:
+                    source_copy(step).wait_send()
         packs = []
         for turn in (first, first + 1):
             owner = flip(k, turn, shards)
@@ -386,8 +473,8 @@
             for half in range(per_shard):
                 tile_sums(pack, half, owner * per_shard + half)
 
-    all_but_one = hists.at[pl.ds(0, device_total - 1)]
-    pltpu.make_async_copy(all_but_one, all_but_one, hist_recv).wait()
+    distant = hists.at[pl.ds(0, groups * (shards - 1))]
+    pltpu.make_async_copy(distant, distant, hist_recv).wait()
     table = jnp.concatenate([hists[d] for d in range(device_total)], axis=0)
     turned[...] = jnp.transpose(table)
     weight = jnp.zeros((source_tiles, nodes), F32)
@@ -402,11 +489,6 @@
         jnp.dot(stack3(irradiance[:, leaves:]), onehot[...], preferred_element_type=F32), 3
     )
     out[...] = irradiance[:, :leaves] + pushed
-
-    pltpu.make_async_copy(all_but_one, all_but_one, hist_send).wait()
-    for step in far_first:
-        if step:
-            source_copy(step).wait_send()
 
 
 def dense_body(
@@ -445,8 +527,10 @@
             pltpu.VMEM((source_tiles, 3, nodes), F32),
             pltpu.SemaphoreType.DMA((shards - 1,)),
             pltpu.SemaphoreType.DMA((shards,)),
+            pltpu.SemaphoreType.DMA((device_total,)),
             pltpu.SemaphoreType.DMA,
-            pltpu.SemaphoreType.DMA,
+            pltpu.SemaphoreType.DMA((device_total,)),
+            pltpu.SemaphoreType.DMA((groups,)),
         ],
         compiler_params=pltpu.CompilerParams(collective_id=0, has_side_effects=True),
     )(*operands, block_count)
@@ -466,6 +550,7 @@
         and nodes // shards <= TILE
         and shards & (shards - 1) == 0
         and shards % 2 == 0
+        and groups & (groups - 1) == 0
         and groups * shards <= TILE
         and slots == TILE
     )

time: 15 us -> 14 us (0.933)
  Pallas kernels: 13.5 us -> 12.5 us
    pallas_call x1, Pallas kernels: 13.5 us -> 12.5 us  [dense_body(): pl.pallas_call(functools.partial(dense_kernel, groups, shards), out_shape...]
where the time goes in v2:
time: 14 us; the launch traced here: 13.8 us
  Pallas kernels  12.5 us (89%)
  between operations  0.69 us (5%)
  other arithmetic  0.6 us (4%)
    pallas_call x1, Pallas kernels, dense_body(): pl.pallas_call(functools.partial(dense_kernel, groups, shards), out_shape...  12.5 us
    add x1, other arithmetic, dense_body(): return leaf_emit + leaf_albedo * gathered  0.6 us

profile of v2, /device:TPU:0, one launch (start us, length us, event | category | flops | bytes accessed | tf_op | source)
XLA Modules:
  0.0 13.8 jit_solution(14245796914886097693)
XLA Ops:
  0.7 0.0 copy-start
  0.7 0.0 copy-start.1
  0.7 12.5 %shard_map.100 = f32[3,512]{1,0:T(4,128)S(1)} custom-call(s32[1,128]{1,0:T(1,128)} %refs_0_.1, s32[1,128]{1,0:T(1,128)} %refs_1_.1, f32[3,512]{1,0:T(4,128)} %refs_2_.1, f32[1,512]{1,0:T(1,128)} %bitcast.2, s32[1,512]{1,0:T(1,128)} %bitcast.3, f32[3,768]{1,0:T(4,128)} %refs_5_.1, f32[2,768]{1,0:T(2,128)} %refs_6_.1, s32[1,1]{1,0:T(1,128)S(6)} %copy.11.refs_7_), custom_call_target="tpu_custom_call" | custom-call | tf_op jit(solution)/shard_map/pallas_call | solution.py:509
  13.2 0.0 copy-done
  13.2 0.0 copy-done.1
  13.2 0.6 %multiply_add_fusion = f32[3,512]{1,0:T(4,128)} fusion(f32[3,512]{1,0:T(4,128)S(1)} %copy-done, f32[3,512]{1,0:T(4,128)S(1)} %copy-done.1, f32[3,512]{1,0:T(4,128)S(1)} %shard_map.100), kind=kLoop, calls=%fused_computation | loop fusion | flops 3072 | bytes 24576 | tf_op jit(solution)/shard_map/add | solution.py:537
Async XLA Ops:
  0.7 12.6 %copy-start = (f32[3,512]{1,0:T(4,128)S(1)}, f32[3,512]{1,0:T(4,128)}, u32[]{:S(2)}) copy-start(f32[3,512]{1,0:T(4,128)} %param.10) | copy-start | bytes 18436
  0.7 12.6 %copy-start.1 = (f32[3,512]{1,0:T(4,128)S(1)}, f32[3,512]{1,0:T(4,128)}, u32[]{:S(2)}) copy-start(f32[3,512]{1,0:T(4,128)} %param.11) | copy-start | bytes 18436

commit v3 on v2

--- a/solution.py
+++ b/solution.py
@@ -226,15 +226,20 @@
             barrier, inc=1, device_id=(group[e], shard), device_id_type=MESH
         )
 
-    for e in reversed(range(groups)):
-
-        @pl.when(clear[e] == 1)
-        def _():
-            lax.fori_loop(0, k, lambda shard, _: (greet(e, shard), 0)[1], 0)
-
-        lax.fori_loop(k + 1, shards, lambda shard, _: (greet(e, shard), 0)[1], 0)
+    def run(first, last, action):
+        lax.fori_loop(first, last, lambda shard, _: (action(shard), 0)[1], 0)
+
+    for e in range(groups):
         if e:
             greet(e, k)
+
+            @pl.when(clear[e] == 1)
+            def _():
+                run(0, k, lambda shard: greet(e, shard))
+
+        else:
+            run(0, k, lambda shard: greet(0, shard))
+        run(k + 1, shards, lambda shard: greet(e, shard))
 
     for copy in loads:
         copy.wait()
@@ -281,7 +286,7 @@
         return pltpu.make_async_remote_copy(
             src_ref=my_hist,
             dst_ref=hists.at[me],
-            send_sem=hist_send.at[e * shards + shard],
+            send_sem=hist_send,
             recv_sem=hist_recv,
             device_id=(group[e], shard),
             device_id_type=MESH,
@@ -291,7 +296,7 @@
         return pltpu.make_async_remote_copy(
             src_ref=my_hist,
             dst_ref=hists.at[me],
-            send_sem=hist_send.at[e * shards + k],
+            send_sem=hist_send,
             recv_sem=peer_recv.at[e],
             device_id=(group[e], k),
             device_id_type=MESH,
@@ -301,7 +306,7 @@
         return pltpu.make_async_remote_copy(
             src_ref=hists.at[group[e] * shards + k],
             dst_ref=hists.at[group[e] * shards + k],
-            send_sem=pass_send.at[e * shards + shard],
+            send_sem=pass_send,
             recv_sem=hist_recv,
             device_id=(g, shard),
             device_id_type=MESH,
@@ -311,20 +316,18 @@
         return pltpu.make_async_remote_copy(
             src_ref=my_pack,
             dst_ref=sources.at[k],
-            send_sem=src_send.at[step - 1],
+            send_sem=src_send,
             recv_sem=src_recv.at[k],
             device_id=(g, flip(k, step, shards)),
             device_id_type=MESH,
         )
 
-    def run(first, last, action):
-        lax.fori_loop(first, last, lambda shard, _: (action(shard), 0)[1], 0)
-
-    for e in reversed(range(groups)):
-        run(0, k, lambda shard: hist_copy(e, shard).start())
+    run(0, k, lambda shard: hist_copy(groups - 1, shard).start())
     for step in far_first:
         if step:
             source_copy(step).start()
+    for e in reversed(range(groups - 1)):
+        run(0, k, lambda shard: hist_copy(e, shard).start())
     for e in range(1, groups):
         peer_copy(e).start()
     for e in range(groups):
@@ -365,7 +368,7 @@
     row8 = lax.broadcasted_iota(jnp.int32, (8, TILE), 0)
     centre8 = jnp.concatenate([middle, jnp.zeros((5, 1), F32)], axis=0)
 
-    def tile_sums(pack, half, tile):
+    def prepare(pack, half, tile):
         values = pack[8 * half : 8 * half + 8, :]
         ratio = pack[8 * per_shard + half : 8 * per_shard + half + 1, :]
         area_here = values[6:7]
@@ -394,6 +397,9 @@
         second, third, less = [
             jnp.broadcast_to(column[:, i : i + 1], (TILE, TILE)) for i in range(3)
         ]
+        return features, second, third, less, tile
+
+    def evaluate(features, second, third, less, tile):
         for pair in range(pairs):
             wide = slice(pair * 2 * TILE, (pair + 1) * 2 * TILE)
             totals = [[None] * 3, [None] * 3]
@@ -422,40 +428,53 @@
                         totals[side][c], axis=0, keepdims=True
                     )
 
+    def rows_done(rows, semaphore):
+        some = hists.at[pl.ds(0, rows)]
+        pltpu.make_async_copy(some, some, semaphore).wait()
+
+    def settle():
+        everything = sources.at[pl.ds(0, shards - 1)]
+        pltpu.make_async_copy(everything, everything, src_send).wait()
+        levels = [1]
+        while levels[-1] < groups:
+            levels.append(2 * levels[-1])
+        for shard in range(shards):
+
+            @pl.when(k == shard)
+            def _():
+                for level in levels:
+                    later = shards - 1 - shard
+                    rows = groups - 1 + groups * shard + later * level
+                    passed = later * (groups - groups // level)
+
+                    @pl.when(drop_total == level)
+                    def _():
+                        rows_done(rows, hist_send)
+                        if passed:
+                            rows_done(passed, pass_send)
+
+    def peer_arrival(e):
+        pltpu.make_async_remote_copy(
+            src_ref=my_hist,
+            dst_ref=hists.at[group[e] * shards + k],
+            send_sem=hist_send,
+            recv_sem=peer_recv.at[e],
+            device_id=(group[e], k),
+            device_id_type=MESH,
+        ).wait_recv()
+
+    held = []
     for first in range(0, shards, 2):
         if first == RELAY_TURN:
             for e in range(1, groups):
-                pltpu.make_async_remote_copy(
-                    src_ref=my_hist,
-                    dst_ref=hists.at[group[e] * shards + k],
-                    send_sem=hist_send.at[0],
-                    recv_sem=peer_recv.at[e],
-                    device_id=(group[e], k),
-                    device_id_type=MESH,
-                ).wait_recv()
 
                 @pl.when(clear[e] == 0)
                 def _():
+                    peer_arrival(e)
                     run(k + 1, shards, lambda shard: passed_copy(e, shard).start())
 
         if first == shards - 2:
-            for e in range(groups):
-                run(0, k, lambda shard: hist_copy(e, shard).wait_send())
-
-                @pl.when(drops[e] == 1)
-                def _():
-                    run(k + 1, shards, lambda shard: hist_copy(e, shard).wait_send())
-
-                if e:
-                    peer_copy(e).wait_send()
-
-                    @pl.when(clear[e] == 0)
-                    def _():
-                        run(k + 1, shards, lambda shard: passed_copy(e, shard).wait_send())
-
-            for step in far_first:
-                if step:
-                    source_copy(step).wait_send()
+            settle()
         packs = []
         for turn in (first, first + 1):
             owner = flip(k, turn, shards)
@@ -463,15 +482,28 @@
                 pltpu.make_async_remote_copy(
                     src_ref=my_pack,
                     dst_ref=sources.at[owner],
-                    send_sem=src_send.at[0],
+                    send_sem=src_send,
                     recv_sem=src_recv.at[owner],
                     device_id=(g, owner),
                     device_id_type=MESH,
                 ).wait_recv()
             packs.append((sources.at[owner] if turn else my_pack, owner))
-        for pack, owner in packs:
-            for half in range(per_shard):
-                tile_sums(pack, half, owner * per_shard + half)
+        ready = [
+            prepare(pack, half, owner * per_shard + half)
+            for pack, owner in packs
+            for half in range(per_shard)
+        ]
+        for tile in held + ready[:-1]:
+            evaluate(*tile)
+        held = ready[-1:]
+    for tile in held:
+        evaluate(*tile)
+
+    for e in range(1, groups):
+
+        @pl.when(clear[e] == 1)
+        def _():
+            peer_arrival(e)
 
     distant = hists.at[pl.ds(0, groups * (shards - 1))]
     pltpu.make_async_copy(distant, distant, hist_recv).wait()
@@ -525,11 +557,11 @@
             pltpu.VMEM((TILE, TILE), F32),
             pltpu.VMEM((TILE, device_total), F32),
             pltpu.VMEM((source_tiles, 3, nodes), F32),
-            pltpu.SemaphoreType.DMA((shards - 1,)),
+            pltpu.SemaphoreType.DMA,
             pltpu.SemaphoreType.DMA((shards,)),
-            pltpu.SemaphoreType.DMA((device_total,)),
             pltpu.SemaphoreType.DMA,
-            pltpu.SemaphoreType.DMA((device_total,)),
+            pltpu.SemaphoreType.DMA,
+            pltpu.SemaphoreType.DMA,
             pltpu.SemaphoreType.DMA((groups,)),
         ],
         compiler_params=pltpu.CompilerParams(collective_id=0, has_side_effects=True),

time: 14 us -> 13.1 us (0.936)
  Pallas kernels: 12.5 us -> 11.6 us
    pallas_call x1, Pallas kernels: 12.5 us -> 11.6 us  [dense_body(): pl.pallas_call(functools.partial(dense_kernel, groups, shards), out_shape...]
where the time goes in v3:
time: 13.1 us; the launch traced here: 12.9 us
  Pallas kernels  11.6 us (89%)
  between operations  0.69 us (5%)
  other arithmetic  0.6 us (5%)
    pallas_call x1, Pallas kernels, dense_body(): pl.pallas_call(functools.partial(dense_kernel, groups, shards), out_shape...  11.6 us
    add x1, other arithmetic, dense_body(): return leaf_emit + leaf_albedo * gathered  0.6 us

profile of v3, /device:TPU:0, one launch (start us, length us, event | category | flops | bytes accessed | tf_op | source)
XLA Modules:
  0.0 12.9 jit_solution(9400431595281241462)
XLA Ops:
  0.7 0.0 copy-start
  0.7 0.0 copy-start.1
  0.7 11.6 %shard_map.100 = f32[3,512]{1,0:T(4,128)S(1)} custom-call(s32[1,128]{1,0:T(1,128)} %refs_0_.1, s32[1,128]{1,0:T(1,128)} %refs_1_.1, f32[3,512]{1,0:T(4,128)} %refs_2_.1, f32[1,512]{1,0:T(1,128)} %bitcast.2, s32[1,512]{1,0:T(1,128)} %bitcast.3, f32[3,768]{1,0:T(4,128)} %refs_5_.1, f32[2,768]{1,0:T(2,128)} %refs_6_.1, s32[1,1]{1,0:T(1,128)S(6)} %copy.11.refs_7_), custom_call_target="tpu_custom_call" | custom-call | tf_op jit(solution)/shard_map/pallas_call | solution.py:541
  12.3 0.0 copy-done
  12.3 0.0 copy-done.1
  12.3 0.6 %multiply_add_fusion = f32[3,512]{1,0:T(4,128)} fusion(f32[3,512]{1,0:T(4,128)S(1)} %copy-done, f32[3,512]{1,0:T(4,128)S(1)} %copy-done.1, f32[3,512]{1,0:T(4,128)S(1)} %shard_map.100), kind=kLoop, calls=%fused_computation | loop fusion | flops 3072 | bytes 24576 | tf_op jit(solution)/shard_map/add | solution.py:569
Async XLA Ops:
  0.7 11.6 %copy-start = (f32[3,512]{1,0:T(4,128)S(1)}, f32[3,512]{1,0:T(4,128)}, u32[]{:S(2)}) copy-start(f32[3,512]{1,0:T(4,128)} %param.10) | copy-start | bytes 18436
  0.7 11.6 %copy-start.1 = (f32[3,512]{1,0:T(4,128)S(1)}, f32[3,512]{1,0:T(4,128)}, u32[]{:S(2)}) copy-start(f32[3,512]{1,0:T(4,128)} %param.11) | copy-start | bytes 18436

commit v4 on v3

--- a/solution.py
+++ b/solution.py
@@ -127,6 +127,7 @@
 NT_DIMS = (((1,), (1,)), ((), ()))
 FEATURES = 8
 RELAY_TURN = 4
+HELD_PAIRS = 1
 ROWS = 64
 
 
@@ -216,7 +217,6 @@
         copy.start()
 
     barrier = pltpu.get_barrier_semaphore()
-    far_first = sorted(range(shards), key=lambda step: -step)
     group = [flip(g, e, groups) for e in range(groups)]
     drops = [all_bits(g, e, groups, True) for e in range(groups)]
     clear = [all_bits(g, e, groups, False) for e in range(groups)]
@@ -312,20 +312,19 @@
             device_id_type=MESH,
         )
 
-    def source_copy(step):
+    def source_copy(shard):
         return pltpu.make_async_remote_copy(
             src_ref=my_pack,
             dst_ref=sources.at[k],
             send_sem=src_send,
             recv_sem=src_recv.at[k],
-            device_id=(g, flip(k, step, shards)),
+            device_id=(g, shard),
             device_id_type=MESH,
         )
 
     run(0, k, lambda shard: hist_copy(groups - 1, shard).start())
-    for step in far_first:
-        if step:
-            source_copy(step).start()
+    run(0, k, lambda shard: source_copy(shard).start())
+    run(k + 1, shards, lambda shard: source_copy(shard).start())
     for e in reversed(range(groups - 1)):
         run(0, k, lambda shard: hist_copy(e, shard).start())
     for e in range(1, groups):
@@ -399,34 +398,41 @@
         ]
         return features, second, third, less, tile
 
-    def evaluate(features, second, third, less, tile):
-        for pair in range(pairs):
-            wide = slice(pair * 2 * TILE, (pair + 1) * 2 * TILE)
-            totals = [[None] * 3, [None] * 3]
-            for first in range(0, TILE, ROWS):
-                some = slice(first, first + ROWS)
-                toward, facing, span = [
-                    jnp.dot(features[some], right[which, :, wide], preferred_element_type=F32)
-                    for which in range(3)
-                ]
-                for side in range(2):
-                    lanes = slice(side * TILE, (side + 1) * TILE)
-                    u = span[:, lanes]
-                    form = (
-                        jnp.maximum(toward[:, lanes], 0.0)
-                        * jnp.maximum(facing[:, lanes], 0.0)
-                        / (u * (u - less[some]))
-                    )
-                    for c, scaled in enumerate((form, form * second[some], form * third[some])):
-                        part = jnp.sum(scaled.reshape(ROWS // 8, 8, TILE), axis=0)
-                        old = totals[side][c]
-                        totals[side][c] = part if old is None else old + part
+    def products(features, pair):
+        wide = slice(pair * 2 * TILE, (pair + 1) * 2 * TILE)
+        return [
+            [
+                jnp.dot(
+                    features[first : first + ROWS], right[which, :, wide],
+                    preferred_element_type=F32,
+                )
+                for which in range(3)
+            ]
+            for first in range(0, TILE, ROWS)
+        ]
+
+    def finish(parts, pair, second, third, less, tile):
+        totals = [[None] * 3, [None] * 3]
+        for first, (toward, facing, span) in zip(range(0, TILE, ROWS), parts):
+            some = slice(first, first + ROWS)
             for side in range(2):
-                first = pair * 2 * TILE + side * TILE
-                for c in range(3):
-                    sums[tile, c : c + 1, first : first + TILE] = jnp.sum(
-                        totals[side][c], axis=0, keepdims=True
-                    )
+                lanes = slice(side * TILE, (side + 1) * TILE)
+                u = span[:, lanes]
+                form = (
+                    jnp.maximum(toward[:, lanes], 0.0)
+                    * jnp.maximum(facing[:, lanes], 0.0)
+                    / (u * (u - less[some]))
+                )
+                for c, scaled in enumerate((form, form * second[some], form * third[some])):
+                    part = jnp.sum(scaled.reshape(ROWS // 8, 8, TILE), axis=0)
+                    old = totals[side][c]
+                    totals[side][c] = part if old is None else old + part
+        for side in range(2):
+            first = pair * 2 * TILE + side * TILE
+            for c in range(3):
+                sums[tile, c : c + 1, first : first + TILE] = jnp.sum(
+                    totals[side][c], axis=0, keepdims=True
+                )
 
     def rows_done(rows, semaphore):
         some = hists.at[pl.ds(0, rows)]
@@ -493,11 +499,16 @@
             for pack, owner in packs
             for half in range(per_shard)
         ]
-        for tile in held + ready[:-1]:
-            evaluate(*tile)
-        held = ready[-1:]
-    for tile in held:
-        evaluate(*tile)
+        for work in held:
+            finish(*work)
+        held = []
+        for number, (features, *rest) in enumerate(ready):
+            for pair in range(pairs):
+                work = (products(features, pair), pair, *rest)
+                if number == len(ready) - 1 and pair >= pairs - HELD_PAIRS:
+                    held.append(work)
+                else:
+                    finish(*work)
 
     for e in range(1, groups):
 
@@ -513,6 +524,8 @@
     for which, tile in enumerate((low_tile, high_tile)):
         rows = turned[pl.ds(pl.multiple_of(tile * source_tiles, 8), source_tiles), :]
         weight += jnp.dot(rows.astype(BF16), place[which], preferred_element_type=F32)
+    for work in held:
+        finish(*work)
 
     irradiance = weight[0:1] * sums[0]
     for tile in range(1, source_tiles):

time: 13.1 us -> 12.7 us (0.969)
  Pallas kernels: 11.6 us -> 11.2 us
    pallas_call x1, Pallas kernels: 11.6 us -> 11.2 us  [dense_body(): pl.pallas_call(functools.partial(dense_kernel, groups, shards), out_shape...]
where the time goes in v4:
time: 12.7 us; the launch traced here: 12.5 us
  Pallas kernels  11.2 us (88%)
  between operations  0.69 us (5%)
  other arithmetic  0.6 us (5%)
    pallas_call x1, Pallas kernels, dense_body(): pl.pallas_call(functools.partial(dense_kernel, groups, shards), out_shape...  11.2 us
    add x1, other arithmetic, dense_body(): return leaf_emit + leaf_albedo * gathered  0.6 us

profile of v4, /device:TPU:0, one launch (start us, length us, event | category | flops | bytes accessed | tf_op | source)
XLA Modules:
  0.0 12.5 jit_solution(14918834964049418501)
XLA Ops:
  0.7 0.0 copy-start
  0.7 0.0 copy-start.1
  0.7 11.2 %shard_map.100 = f32[3,512]{1,0:T(4,128)S(1)} custom-call(s32[1,128]{1,0:T(1,128)} %refs_0_.1, s32[1,128]{1,0:T(1,128)} %refs_1_.1, f32[3,512]{1,0:T(4,128)} %refs_2_.1, f32[1,512]{1,0:T(1,128)} %bitcast.2, s32[1,512]{1,0:T(1,128)} %bitcast.3, f32[3,768]{1,0:T(4,128)} %refs_5_.1, f32[2,768]{1,0:T(2,128)} %refs_6_.1, s32[1,1]{1,0:T(1,128)S(6)} %copy.11.refs_7_), custom_call_target="tpu_custom_call" | custom-call | tf_op jit(solution)/shard_map/pallas_call | solution.py:554
  11.9 0.0 copy-done
  11.9 0.0 copy-done.1
  11.9 0.6 %multiply_add_fusion = f32[3,512]{1,0:T(4,128)} fusion(f32[3,512]{1,0:T(4,128)S(1)} %copy-done, f32[3,512]{1,0:T(4,128)S(1)} %copy-done.1, f32[3,512]{1,0:T(4,128)S(1)} %shard_map.100), kind=kLoop, calls=%fused_computation | loop fusion | flops 3072 | bytes 24576 | tf_op jit(solution)/shard_map/add | solution.py:582
Async XLA Ops:
  0.7 11.2 %copy-start = (f32[3,512]{1,0:T(4,128)S(1)}, f32[3,512]{1,0:T(4,128)}, u32[]{:S(2)}) copy-start(f32[3,512]{1,0:T(4,128)} %param.10) | copy-start | bytes 18436
  0.7 11.2 %copy-start.1 = (f32[3,512]{1,0:T(4,128)S(1)}, f32[3,512]{1,0:T(4,128)}, u32[]{:S(2)}) copy-start(f32[3,512]{1,0:T(4,128)} %param.11) | copy-start | bytes 18436

commit v5 on v4

--- a/solution.py
+++ b/solution.py
@@ -191,7 +191,7 @@
 
 def dense_kernel(groups, shards, *refs):
     operands, count, out, inputs, scratch = refs[:7], refs[7], refs[8], refs[9:16], refs[16:]
-    receiver_id, source_id, radiosity, area, parent, position, angles = inputs
+    receiver_id, source_id, area, parent, angles, radiosity, position = inputs
     (
         load,
         sources, my_pack, my_hist, hists, right, onehot, place, columns, turned, sums,
@@ -211,7 +211,8 @@
     pairs = nodes // (2 * TILE)
 
     loads = [
-        pltpu.make_async_copy(operands[i], inputs[i], load.at[i]) for i in range(len(inputs))
+        pltpu.make_async_copy(operands[i], inputs[i], load.at[max(i - 4, 0)])
+        for i in range(len(inputs))
     ]
     for copy in loads:
         copy.start()
@@ -221,6 +222,10 @@
     drops = [all_bits(g, e, groups, True) for e in range(groups)]
     clear = [all_bits(g, e, groups, False) for e in range(groups)]
 
+    def rows_done(rows, semaphore):
+        some = hists.at[pl.ds(0, rows)]
+        pltpu.make_async_copy(some, some, semaphore).wait()
+
     def greet(e, shard):
         pl.semaphore_signal(
             barrier, inc=1, device_id=(group[e], shard), device_id_type=MESH
@@ -229,19 +234,13 @@
     def run(first, last, action):
         lax.fori_loop(first, last, lambda shard, _: (action(shard), 0)[1], 0)
 
-    for e in range(groups):
-        if e:
-            greet(e, k)
-
-            @pl.when(clear[e] == 1)
-            def _():
-                run(0, k, lambda shard: greet(e, shard))
-
-        else:
-            run(0, k, lambda shard: greet(0, shard))
-        run(k + 1, shards, lambda shard: greet(e, shard))
-
-    for copy in loads:
+    for step in range(1, shards):
+        greet(0, flip(k, step, shards))
+    for e in reversed(range(1, groups)):
+        run(k * (1 - clear[e]), shards, lambda shard: greet(e, shard))
+
+    rows_done(sum(x.size for x in inputs[:5]) // TILE, load.at[0])
+    for copy in loads[5:]:
         copy.wait()
 
     lane = lax.broadcasted_iota(jnp.int32, (1, TILE), 1)
@@ -297,7 +296,7 @@
             src_ref=my_hist,
             dst_ref=hists.at[me],
             send_sem=hist_send,
-            recv_sem=peer_recv.at[e],
+            recv_sem=peer_recv.at[e - 1],
             device_id=(group[e], k),
             device_id_type=MESH,
         )
@@ -317,7 +316,7 @@
             src_ref=my_pack,
             dst_ref=sources.at[k],
             send_sem=src_send,
-            recv_sem=src_recv.at[k],
+            recv_sem=src_recv.at[k // 2],
             device_id=(g, shard),
             device_id_type=MESH,
         )
@@ -430,13 +429,7 @@
         for side in range(2):
             first = pair * 2 * TILE + side * TILE
             for c in range(3):
-                sums[tile, c : c + 1, first : first + TILE] = jnp.sum(
-                    totals[side][c], axis=0, keepdims=True
-                )
-
-    def rows_done(rows, semaphore):
-        some = hists.at[pl.ds(0, rows)]
-        pltpu.make_async_copy(some, some, semaphore).wait()
+                sums[tile, c, :, first : first + TILE] = totals[side][c]
 
     def settle():
         everything = sources.at[pl.ds(0, shards - 1)]
@@ -464,7 +457,7 @@
             src_ref=my_hist,
             dst_ref=hists.at[group[e] * shards + k],
             send_sem=hist_send,
-            recv_sem=peer_recv.at[e],
+            recv_sem=peer_recv.at[e - 1],
             device_id=(group[e], k),
             device_id_type=MESH,
         ).wait_recv()
@@ -481,19 +474,15 @@
 
         if first == shards - 2:
             settle()
-        packs = []
-        for turn in (first, first + 1):
-            owner = flip(k, turn, shards)
-            if turn:
-                pltpu.make_async_remote_copy(
-                    src_ref=my_pack,
-                    dst_ref=sources.at[owner],
-                    send_sem=src_send,
-                    recv_sem=src_recv.at[owner],
-                    device_id=(g, owner),
-                    device_id_type=MESH,
-                ).wait_recv()
-            packs.append((sources.at[owner] if turn else my_pack, owner))
+        owners = [flip(k, first, shards), flip(k, first + 1, shards)]
+        if first:
+            both = sources.at[pl.ds(owners[0] // 2 * 2, 2)]
+        else:
+            both = sources.at[owners[1]]
+        pltpu.make_async_copy(both, both, src_recv.at[owners[0] // 2]).wait()
+        packs = [(sources.at[owner], owner) for owner in owners]
+        if not first:
+            packs[0] = (my_pack, k)
         ready = [
             prepare(pack, half, owner * per_shard + half)
             for pack, owner in packs
@@ -527,9 +516,19 @@
     for work in held:
         finish(*work)
 
-    irradiance = weight[0:1] * sums[0]
-    for tile in range(1, source_tiles):
-        irradiance += weight[tile : tile + 1] * sums[tile]
+    chunk_rows = []
+    for chunk in range(chunks):
+        lanes = slice(chunk * TILE, (chunk + 1) * TILE)
+        totals = [None] * 3
+        for tile in range(source_tiles):
+            scale = jnp.broadcast_to(weight[tile : tile + 1, lanes], (8, TILE))
+            for c in range(3):
+                part = scale * sums[tile, c, :, lanes]
+                totals[c] = part if totals[c] is None else totals[c] + part
+        chunk_rows.append(
+            jnp.concatenate([jnp.sum(x, axis=0, keepdims=True) for x in totals], axis=0)
+        )
+    irradiance = jnp.concatenate(chunk_rows, axis=1)
     pushed = unstack3(
         jnp.dot(stack3(irradiance[:, leaves:]), onehot[...], preferred_element_type=F32), 3
     )
@@ -547,8 +546,8 @@
     source_tiles = shards * per_shard
     device_total = groups * shards
     operands = (
-        block_receiver, block_source, leaf_radiosity, leaf_area[None, :], parent_index[None, :],
-        node_position, node_angles,
+        block_receiver, block_source, leaf_area[None, :], parent_index[None, :], node_angles,
+        leaf_radiosity, node_position,
     )
     pack_rows = 9 * per_shard
     gathered = pl.pallas_call(
@@ -559,7 +558,7 @@
         out_specs=pl.BlockSpec(memory_space=pltpu.VMEM),
         scratch_shapes=[pltpu.VMEM(x.shape, x.dtype) for x in operands]
         + [
-            pltpu.SemaphoreType.DMA((len(operands),)),
+            pltpu.SemaphoreType.DMA((len(operands) - 4,)),
             pltpu.VMEM((shards, pack_rows, TILE), F32),
             pltpu.VMEM((pack_rows, TILE), F32),
             pltpu.VMEM((1, TILE), F32),
@@ -569,13 +568,13 @@
             pltpu.VMEM((2, device_total, nodes), BF16),
             pltpu.VMEM((TILE, TILE), F32),
             pltpu.VMEM((TILE, device_total), F32),
-            pltpu.VMEM((source_tiles, 3, nodes), F32),
+            pltpu.VMEM((source_tiles, 3, 8, nodes), F32),
             pltpu.SemaphoreType.DMA,
-            pltpu.SemaphoreType.DMA((shards,)),
+            pltpu.SemaphoreType.DMA((shards // 2,)),
             pltpu.SemaphoreType.DMA,
             pltpu.SemaphoreType.DMA,
             pltpu.SemaphoreType.DMA,
-            pltpu.SemaphoreType.DMA((groups,)),
+            pltpu.SemaphoreType.DMA((groups - 1,)),
         ],
         compiler_params=pltpu.CompilerParams(collective_id=0, has_side_effects=True),
     )(*operands, block_count)
@@ -591,6 +590,8 @@
         and TILE % source_tiles == 0
         and source_tiles % 8 == 0
         and nodes % (2 * TILE) == 0
+        and leaves % TILE == 0
+        and groups > 1
         and nodes % shards == 0
         and nodes // shards <= TILE
         and shards & (shards - 1) == 0

time: 12.7 us -> 12.4 us (0.976)
  Pallas kernels: 11.2 us -> 11 us
    pallas_call x1, Pallas kernels: 11.2 us -> 11 us  [dense_body(): pl.pallas_call(functools.partial(dense_kernel, groups, shards), out_shape...]
where the time goes in v5:
time: 12.4 us; the launch traced here: 12.3 us
  Pallas kernels  11 us (89%)
  between operations  0.69 us (6%)
  other arithmetic  0.6 us (5%)
    pallas_call x1, Pallas kernels, dense_body(): pl.pallas_call(functools.partial(dense_kernel, groups, shards), out_shape...  11 us
    add x1, other arithmetic, dense_body(): return leaf_emit + leaf_albedo * gathered  0.6 us

profile of v5, /device:TPU:0, one launch (start us, length us, event | category | flops | bytes accessed | tf_op | source)
XLA Modules:
  0.0 12.3 jit_solution(6609470568022640166)
XLA Ops:
  0.7 0.0 copy-start
  0.7 0.0 copy-start.1
  0.7 11.0 %shard_map.100 = f32[3,512]{1,0:T(4,128)S(1)} custom-call(s32[1,128]{1,0:T(1,128)} %refs_0_.1, s32[1,128]{1,0:T(1,128)} %refs_1_.1, f32[1,512]{1,0:T(1,128)} %bitcast.2, s32[1,512]{1,0:T(1,128)} %bitcast.3, f32[2,768]{1,0:T(2,128)} %refs_4_.1, f32[3,512]{1,0:T(4,128)} %refs_5_.1, f32[3,768]{1,0:T(4,128)} %refs_6_.1, s32[1,1]{1,0:T(1,128)S(6)} %copy.11.refs_7_), custom_call_target="tpu_custom_call" | custom-call | tf_op jit(solution)/shard_map/pallas_call | solution.py:553
  11.6 0.0 copy-done
  11.7 0.0 copy-done.1
  11.7 0.6 %multiply_add_fusion = f32[3,512]{1,0:T(4,128)} fusion(f32[3,512]{1,0:T(4,128)S(1)} %copy-done, f32[3,512]{1,0:T(4,128)S(1)} %copy-done.1, f32[3,512]{1,0:T(4,128)S(1)} %shard_map.100), kind=kLoop, calls=%fused_computation | loop fusion | flops 3072 | bytes 24576 | tf_op jit(solution)/shard_map/add | solution.py:581
Async XLA Ops:
  0.7 11.0 %copy-start = (f32[3,512]{1,0:T(4,128)S(1)}, f32[3,512]{1,0:T(4,128)}, u32[]{:S(2)}) copy-start(f32[3,512]{1,0:T(4,128)} %param.10) | copy-start | bytes 18436
  0.7 11.0 %copy-start.1 = (f32[3,512]{1,0:T(4,128)S(1)}, f32[3,512]{1,0:T(4,128)}, u32[]{:S(2)}) copy-start(f32[3,512]{1,0:T(4,128)} %param.11) | copy-start | bytes 18436

commit v6 on v5

--- a/solution.py
+++ b/solution.py
@@ -321,9 +321,11 @@
             device_id_type=MESH,
         )
 
-    run(0, k, lambda shard: hist_copy(groups - 1, shard).start())
+    urgent = jnp.minimum(k, 2)
+    run(0, urgent, lambda shard: hist_copy(groups - 1, shard).start())
     run(0, k, lambda shard: source_copy(shard).start())
     run(k + 1, shards, lambda shard: source_copy(shard).start())
+    run(urgent, k, lambda shard: hist_copy(groups - 1, shard).start())
     for e in reversed(range(groups - 1)):
         run(0, k, lambda shard: hist_copy(e, shard).start())
     for e in range(1, groups):

time: 12.4 us -> 12.4 us (level)
  no operation moved by 1% of the time
where the time goes in v6:
time: 12.4 us; the launch traced here: 12.2 us
  Pallas kernels  10.9 us (88%)
  between operations  0.69 us (6%)
  other arithmetic  0.6 us (5%)
    pallas_call x1, Pallas kernels, dense_body(): pl.pallas_call(functools.partial(dense_kernel, groups, shards), out_shape...  10.9 us
    add x1, other arithmetic, dense_body(): return leaf_emit + leaf_albedo * gathered  0.6 us

profile of v6, /device:TPU:0, one launch (start us, length us, event | category | flops | bytes accessed | tf_op | source)
XLA Modules:
  0.0 12.2 jit_solution(7322373750328682911)
XLA Ops:
  0.7 0.0 copy-start
  0.7 0.0 copy-start.1
  0.7 10.9 %shard_map.100 = f32[3,512]{1,0:T(4,128)S(1)} custom-call(s32[1,128]{1,0:T(1,128)} %refs_0_.1, s32[1,128]{1,0:T(1,128)} %refs_1_.1, f32[1,512]{1,0:T(1,128)} %bitcast.2, s32[1,512]{1,0:T(1,128)} %bitcast.3, f32[2,768]{1,0:T(2,128)} %refs_4_.1, f32[3,512]{1,0:T(4,128)} %refs_5_.1, f32[3,768]{1,0:T(4,128)} %refs_6_.1, s32[1,1]{1,0:T(1,128)S(6)} %copy.11.refs_7_), custom_call_target="tpu_custom_call" | custom-call | tf_op jit(solution)/shard_map/pallas_call | solution.py:555
  11.6 0.0 copy-done
  11.6 0.0 copy-done.1
  11.6 0.6 %multiply_add_fusion = f32[3,512]{1,0:T(4,128)} fusion(f32[3,512]{1,0:T(4,128)S(1)} %copy-done, f32[3,512]{1,0:T(4,128)S(1)} %copy-done.1, f32[3,512]{1,0:T(4,128)S(1)} %shard_map.100), kind=kLoop, calls=%fused_computation | loop fusion | flops 3072 | bytes 24576 | tf_op jit(solution)/shard_map/add | solution.py:583
Async XLA Ops:
  0.7 11.0 %copy-start = (f32[3,512]{1,0:T(4,128)S(1)}, f32[3,512]{1,0:T(4,128)}, u32[]{:S(2)}) copy-start(f32[3,512]{1,0:T(4,128)} %param.10) | copy-start | bytes 18436
  0.7 11.0 %copy-start.1 = (f32[3,512]{1,0:T(4,128)S(1)}, f32[3,512]{1,0:T(4,128)}, u32[]{:S(2)}) copy-start(f32[3,512]{1,0:T(4,128)} %param.11) | copy-start | bytes 18436

commit v7 on v5

--- a/solution.py
+++ b/solution.py
@@ -507,7 +507,7 @@
 
     distant = hists.at[pl.ds(0, groups * (shards - 1))]
     pltpu.make_async_copy(distant, distant, hist_recv).wait()
-    table = jnp.concatenate([hists[d] for d in range(device_total)], axis=0)
+    table = hists[...].reshape(device_total, TILE)
     turned[...] = jnp.transpose(table)
     weight = jnp.zeros((source_tiles, nodes), F32)
     for which, tile in enumerate((low_tile, high_tile)):

time: 12.4 us -> 12.4 us (level)
  no operation moved by 1% of the time
where the time goes in v7:
time: 12.4 us; the launch traced here: 12.3 us
  Pallas kernels  11 us (89%)
  between operations  0.69 us (6%)
  other arithmetic  0.6 us (5%)
    pallas_call x1, Pallas kernels, dense_body(): pl.pallas_call(functools.partial(dense_kernel, groups, shards), out_shape...  11 us
    add x1, other arithmetic, dense_body(): return leaf_emit + leaf_albedo * gathered  0.6 us

profile of v7, /device:TPU:0, one launch (start us, length us, event | category | flops | bytes accessed | tf_op | source)
XLA Modules:
  0.0 12.3 jit_solution(14266863480048008456)
XLA Ops:
  0.7 0.0 copy-start
  0.7 0.0 copy-start.1
  0.7 11.0 %shard_map.100 = f32[3,512]{1,0:T(4,128)S(1)} custom-call(s32[1,128]{1,0:T(1,128)} %refs_0_.1, s32[1,128]{1,0:T(1,128)} %refs_1_.1, f32[1,512]{1,0:T(1,128)} %bitcast.2, s32[1,512]{1,0:T(1,128)} %bitcast.3, f32[2,768]{1,0:T(2,128)} %refs_4_.1, f32[3,512]{1,0:T(4,128)} %refs_5_.1, f32[3,768]{1,0:T(4,128)} %refs_6_.1, s32[1,1]{1,0:T(1,128)S(6)} %copy.11.refs_7_), custom_call_target="tpu_custom_call" | custom-call | tf_op jit(solution)/shard_map/pallas_call | solution.py:553
  11.6 0.0 copy-done
  11.7 0.0 copy-done.1
  11.7 0.6 %multiply_add_fusion = f32[3,512]{1,0:T(4,128)} fusion(f32[3,512]{1,0:T(4,128)S(1)} %copy-done, f32[3,512]{1,0:T(4,128)S(1)} %copy-done.1, f32[3,512]{1,0:T(4,128)S(1)} %shard_map.100), kind=kLoop, calls=%fused_computation | loop fusion | flops 3072 | bytes 24576 | tf_op jit(solution)/shard_map/add | solution.py:581
Async XLA Ops:
  0.7 11.0 %copy-start = (f32[3,512]{1,0:T(4,128)S(1)}, f32[3,512]{1,0:T(4,128)}, u32[]{:S(2)}) copy-start(f32[3,512]{1,0:T(4,128)} %param.10) | copy-start | bytes 18436
  0.7 11.0 %copy-start.1 = (f32[3,512]{1,0:T(4,128)S(1)}, f32[3,512]{1,0:T(4,128)}, u32[]{:S(2)}) copy-start(f32[3,512]{1,0:T(4,128)} %param.11) | copy-start | bytes 18436
